TPU v7x, 32 devices: a whole 2x2x4 slice. The times are simulated.
32 devices in a mesh: dp: 4 (over z), vocab: 8 (over y, x, core).
Axes of the slice: x: 2, y: 2, z: 4, core: 2. Of those that a mesh axis runs over, the one named last changes fastest.
Arguments:
- teacher_logits: bfloat16 [1536, 151552], P('dp', 'vocab'), may hold values from -40 to 320, as said below
- student_logits: bfloat16 [1536, 126976], P('dp', 'vocab'), may hold values from -40 to 320, as said below
- tile_dest: int32 [1184, 2], replicated, may hold values from 0 to 991, as said below
- tile_weight: bfloat16 [1184, 2, 128, 128], P('vocab'), may hold values from 0.0009994507 to 1
- token_mask: int32 [1536], P('dp'), may hold values from 0 to 1, as said below
Outputs:
- token_loss: float32 [1536], P('dp')
- mean_loss: float32 [], replicated
Inputs may be any that keep to these rules, and one draw needn't show every extreme that they name: `teacher_logits`: Real-valued logits. `student_logits`: Real-valued logits. `tile_dest`: row b names the student blocks of the 2 tiles of teacher block b. Student block s belongs to vocab index s // 124, teacher block b to vocab index b // 148. Of the tiles of the teacher blocks of one vocab index, at most 37 name student blocks of any one vocab index, and exactly 37 do for some vocab index. `token_mask`: at least one token has a 1.
All inputs are finite; a program needn't handle non-finite values.
Results may differ from a plain program's by a relative error of at most 0.0031.
Values may be sent and summed in bfloat16 or wider, within the bound.
A program may use at most 192 MiB of HBM per device.

v0:
```python
import functools
import math

import jax
import jax.numpy as jnp
from jax import lax
from jax.experimental import pallas as pl
from jax.experimental.pallas import tpu as pltpu
from jax.sharding import PartitionSpec as P

BLOCK = 128
SMOOTH = 0.1
CHUNK = 96
F32 = jnp.float32
BF16 = jnp.bfloat16


def kernel(n, ndp, cap, tbd, sbd, chunk, nc, c0, sidx, sblk, rord, rblk, rsrc, keep, last, valid,
           inv_ref, mask_ref, t_hbm, s_hbm, w_hbm, loss_ref, mean_ref,
           tbuf, stbuf, wbuf, prob, sbuf, rbuf0, rbuf1, st_send, st_recv, tr, scl, smx, xbuf,
           fsend, frecv, dsend, drecv,
           in_sem, send_sem, recv_sem, sts_sem, str_sem, fs_sem, fr_sem, ds_sem, dr_sem, credit):
    me = lax.axis_index("vocab")
    slots = n * cap
    rbuf = (rbuf0, rbuf1)
    order = list(range(2, n, 2)) + list(range(3, n, 2)) + [1]
    peers = [me ^ j for j in order]
    my_dp = lax.axis_index("dp")
    dp_peers = [lax.rem(my_dp + j, ndp) for j in range(1, ndp)]
    shape = (chunk, BLOCK)
    zeros = jnp.zeros(shape, F32)
    lane = lax.broadcasted_iota(jnp.int32, shape, 1)

    def cols(b):
        return pl.ds(pl.multiple_of(b * BLOCK, BLOCK), BLOCK)

    def load_t(c):
        return pltpu.make_async_copy(t_hbm.at[pl.ds(c * chunk, chunk)], tbuf, in_sem.at[0])

    def load_s(c):
        return pltpu.make_async_copy(s_hbm.at[pl.ds(c * chunk, chunk)], stbuf, in_sem.at[1])

    load_w = pltpu.make_async_copy(w_hbm, wbuf, in_sem.at[2])
    load_t(0).start()
    load_w.start()

    barrier = pltpu.get_barrier_semaphore()
    for d in peers:
        pl.semaphore_signal(barrier, inc=1, device_id={"vocab": d})
    for e in dp_peers:
        pl.semaphore_signal(barrier, inc=1, device_id={"dp": e})
    pl.semaphore_wait(barrier, n + ndp - 2)

    tr[...] = jnp.zeros_like(tr)

    def tile_copy(par, d):
        return pltpu.make_async_remote_copy(
            src_ref=sbuf.at[par, d], dst_ref=rbuf[par].at[pl.ds(me * cap, cap)],
            send_sem=send_sem.at[par, d], recv_sem=recv_sem.at[par, me],
            device_id={"vocab": d})

    def tile_wait(par, src):
        return pltpu.make_async_remote_copy(
            src_ref=sbuf.at[par, src], dst_ref=rbuf[par].at[pl.ds(src * cap, cap)],
            send_sem=send_sem.at[par, src], recv_sem=recv_sem.at[par, src],
            device_id={"vocab": src})

    def stat_copy(par, d):
        return pltpu.make_async_remote_copy(
            src_ref=st_send.at[par], dst_ref=st_recv.at[par, me],
            send_sem=sts_sem.at[par, d], recv_sem=str_sem.at[par, me],
            device_id={"vocab": d})

    def stat_wait(par, src):
        return pltpu.make_async_remote_copy(
            src_ref=st_send.at[par], dst_ref=st_recv.at[par, src],
            send_sem=sts_sem.at[par, src], recv_sem=str_sem.at[par, src],
            device_id={"vocab": src})

    def bcast(column):
        return jnp.broadcast_to(column, shape)

    def turned(stat):
        if chunk < BLOCK:
            stat = jnp.concatenate([stat, jnp.zeros((BLOCK - chunk, BLOCK), F32)], axis=0)
        return stat.T[:8]

    def produce(c):
        par = c % 2
        load_t(c).wait()
        tmax = lax.fori_loop(
            0, tbd, lambda b, m: jnp.maximum(m, tbuf[:, cols(b)].astype(F32)),
            jnp.full(shape, -jnp.inf, F32), unroll=2)
        tmax = bcast(jnp.max(tmax, axis=1, keepdims=True))

        def expo(b, total):
            e = jnp.exp(tbuf[:, cols(b)].astype(F32) - tmax)
            prob[b] = (e * inv_ref[pl.ds(b, 1), :]).astype(BF16)
            return total + e

        total = lax.fori_loop(0, tbd, expo, zeros, unroll=2)
        if c + 1 < nc:
            load_t(c + 1).start()
        tsum = bcast(jnp.sum(total, axis=1, keepdims=True))
        stat = jnp.where(lane == 0, tmax, jnp.where(lane == 1, tsum, 0.0))
        if c >= 2:
            for d in peers:
                stat_copy(par, d).wait_send()
        rows = turned(stat)
        st_send[par] = rows
        st_recv[par, me] = rows
        if c == 0:
            load_w.wait()

        def compute(d, dst):
            def one(r, carry):
                i = sidx[d * cap + r]
                b = sblk[d * cap + r]
                dst[r] = jnp.dot(prob[b], wbuf[i], preferred_element_type=F32).astype(BF16)
                return carry
            lax.fori_loop(0, cap, one, 0, unroll=4)

        for d in peers:
            if c >= 2:
                tile_copy(par, d).wait_send()
            compute(d, sbuf.at[par, d])
            if c >= 2:
                pl.semaphore_wait(credit.at[d], 1)
            stat_copy(par, d).start()
            tile_copy(par, d).start()
        compute(me, rbuf[par].at[pl.ds(me * cap, cap)])

    def student(c):
        load_s(c).wait()
        m = lax.fori_loop(
            0, sbd, lambda b, m: jnp.maximum(m, stbuf[:, cols(b)].astype(F32)),
            jnp.full(shape, -jnp.inf, F32), unroll=2)
        m = bcast(jnp.max(m, axis=1, keepdims=True))
        smx[...] = m

        def step(b, carry):
            total, lin = carry
            x = stbuf[:, cols(b)].astype(F32) - m
            xbuf[b] = x
            return total + jnp.exp(x), lin + x

        total, lin = lax.fori_loop(0, sbd, step, (zeros, zeros), unroll=2)
        if c + 1 < nc:
            load_s(c + 1).start()
        return (jnp.sum(total, axis=1, keepdims=True), jnp.sum(lin, axis=1, keepdims=True))

    def consume(c):
        par = c % 2
        ssum, slin = student(c)
        for d in peers:
            stat_wait(par, d).wait_recv()
        groups = (n * 8 + BLOCK - 1) // BLOCK
        per = BLOCK // 8
        columns = []
        for g in range(groups):
            for j in range(min(per, n - g * per)):
                tr[j * 8:j * 8 + 8, :] = st_recv[par, g * per + j]
            block = tr[...].T
            for j in range(min(per, n - g * per)):
                columns.append((block[:chunk, 8 * j:8 * j + 1], block[:chunk, 8 * j + 1:8 * j + 2]))
        gmax = functools.reduce(jnp.maximum, [m for m, _ in columns])
        gsum = sum(s * jnp.exp(m - gmax) for m, s in columns)
        for j, (m, _) in enumerate(columns):
            scl[j] = bcast(jnp.exp(m - gmax) / gsum)
        for d in peers:
            tile_wait(par, d).wait_recv()
        clogc = c0 * math.log(c0)

        def step(i, carry):
            acc, mass, lin, ent = carry
            o = rord[i]
            src = rsrc[i]
            t = rbuf[par][o].astype(F32) * (scl[src] * valid[i])
            x = xbuf[rblk[i]]
            acc = acc * keep[i] + t
            tgt = (1.0 - SMOOTH) * acc + c0
            ent = ent + last[i] * (tgt * jnp.log(tgt) - clogc)
            return acc, mass + t, lin + t * x, ent

        _, mass, lin, ent = lax.fori_loop(0, slots, step, (zeros,) * 4, unroll=2)
        mass, lin, ent = [jnp.sum(v, axis=1, keepdims=True) for v in (mass, lin, ent)]
        count = sbd * BLOCK
        kla = ent + count * clogc - (1.0 - SMOOTH) * lin - c0 * slin
        tot = (1.0 - SMOOTH) * mass + count * c0
        fsend[c * 8:c * 8 + 8, :] = turned(jnp.where(
            lane == 0, kla, jnp.where(lane == 1, tot, jnp.where(lane == 2, smx[...], ssum))))
        if c + 2 < nc:
            for d in peers:
                pl.semaphore_signal(credit.at[me], inc=1, device_id={"vocab": d})

    load_s(0).start()
    for c in range(nc):
        produce(c)
        if c >= 1:
            consume(c - 1)
    consume(nc - 1)
    def fin_copy(d, src):
        return pltpu.make_async_remote_copy(
            src_ref=fsend, dst_ref=frecv.at[src], send_sem=fs_sem.at[d],
            recv_sem=fr_sem.at[src], device_id={"vocab": d})

    def dp_copy(e, src):
        return pltpu.make_async_remote_copy(
            src_ref=dsend, dst_ref=drecv.at[src], send_sem=ds_sem.at[e],
            recv_sem=dr_sem.at[src], device_id={"dp": e})

    for d in peers:
        fin_copy(d, me).start()
    frecv[me] = fsend[...]
    for d in peers:
        fin_copy(d, d).wait_recv()
    real = lax.broadcasted_iota(jnp.int32, (1, BLOCK), 1) < chunk
    dsend[...] = jnp.zeros_like(dsend)
    for c in range(nc):
        parts = [frecv[v, c * 8:c * 8 + 8, :] for v in range(n)]
        gmax = functools.reduce(jnp.maximum, [p[2:3] for p in parts])
        lse = gmax + jnp.log(sum(p[3:4] * jnp.exp(p[2:3] - gmax) for p in parts))
        kl = sum(p[0:1] + p[1:2] * (lse - p[2:3]) for p in parts)
        mask = mask_ref[c:c + 1, :]
        loss = mask * jnp.where(real, kl, 0.0)
        loss_ref[c:c + 1, :] = loss
        dsend[0:1, :] += loss
        dsend[1:2, :] += mask
    for e in dp_peers:
        dp_copy(e, my_dp).start()
    drecv[my_dp] = dsend[...]
    for e in dp_peers:
        dp_copy(e, e).wait_recv()
    sums = sum(drecv[v] for v in range(ndp))
    mean_ref[...] = jnp.broadcast_to(
        jnp.sum(sums[0:1], axis=1, keepdims=True) / jnp.sum(sums[1:2], axis=1, keepdims=True),
        (8, BLOCK))
    for d in peers:
        fin_copy(d, d).wait_send()
    for e in dp_peers:
        dp_copy(e, e).wait_send()
    for c in range(max(nc - 2, 0), nc):
        for d in peers:
            stat_copy(c % 2, d).wait_send()
            tile_copy(c % 2, d).wait_send()


def tables(tile_dest, n, cap, tbd, sbd, me):
    per = tbd * tile_dest.shape[1]
    dest = tile_dest.reshape(n, per)
    owner = dest // sbd
    block = dest % sbd
    i32 = jnp.int32
    before = jnp.arange(per)[:, None] < jnp.arange(per)[None, :]
    mine = lax.dynamic_index_in_dim(owner, me, 0, keepdims=False)
    rank = jnp.sum((mine[:, None] == mine[None, :]) & before, axis=0, dtype=i32)
    slot = mine * cap + rank
    hit = slot[:, None] == jnp.arange(n * cap)[None, :]
    sidx = jnp.sum(jnp.where(hit, jnp.arange(per, dtype=i32)[:, None], 0), axis=0)
    here = owner == me
    rrank = jnp.sum(here[:, :, None] & before[None], axis=1, dtype=i32)
    rhit = here[:, :, None] & (rrank[:, :, None] == jnp.arange(cap))
    rb = jnp.sum(jnp.where(rhit, block[:, :, None] + 1, 0), axis=1).reshape(-1)
    k = n * cap
    ids = jnp.arange(k, dtype=i32)
    key = jnp.where(rb > 0, rb - 1, sbd) * k + ids
    pos = jnp.sum(key[None, :] < key[:, None], axis=1, dtype=i32)
    order = jnp.sum(jnp.where(pos[:, None] == ids[None, :], key[:, None], 0), axis=0)
    blk = order // k
    o = order % k
    valid = (blk < sbd).astype(F32)
    same = blk[1:] == blk[:-1]
    edge = jnp.zeros((1,), bool)
    keep = jnp.concatenate([edge, same]).astype(F32)
    last = (1.0 - jnp.concatenate([same, edge]).astype(F32)) * valid
    return sidx, sidx // tile_dest.shape[1], o, jnp.minimum(blk, sbd - 1), o // cap, keep, last, valid


def local(teacher_logits, student_logits, tile_dest, tile_weight, token_mask):
    n = lax.axis_size("vocab")
    ndp = lax.axis_size("dp")
    me = lax.axis_index("vocab")
    rows = teacher_logits.shape[0]
    tbd = teacher_logits.shape[1] // BLOCK
    sbd = student_logits.shape[1] // BLOCK
    k = tile_dest.shape[1]
    cap = (tbd * k + n - 1) // n
    chunk = math.gcd(rows, CHUNK)
    nc = rows // chunk
    c0 = SMOOTH / (sbd * BLOCK * n)
    tabs = tables(tile_dest, n, cap, tbd, sbd, me)
    inv = 1.0 / jnp.sum(tile_weight.astype(F32), axis=(1, 3))
    weights = tile_weight.reshape(tbd * k, BLOCK, BLOCK)
    smem = pl.BlockSpec(memory_space=pltpu.SMEM)
    anyspec = pl.BlockSpec(memory_space=pl.ANY)
    vmem = pl.BlockSpec(memory_space=pltpu.VMEM)
    dma = pltpu.SemaphoreType.DMA
    mask = jnp.pad(token_mask.astype(F32).reshape(nc, chunk), ((0, 0), (0, BLOCK - chunk)))
    loss, mean = pl.pallas_call(
        functools.partial(kernel, n, ndp, cap, tbd, sbd, chunk, nc, c0),
        out_shape=[jax.ShapeDtypeStruct((nc, BLOCK), F32), jax.ShapeDtypeStruct((8, BLOCK), F32)],
        in_specs=[smem] * 8 + [vmem] * 2 + [anyspec] * 3,
        out_specs=[vmem] * 2,
        scratch_shapes=[
            pltpu.VMEM((chunk, tbd * BLOCK), BF16),
            pltpu.VMEM((chunk, sbd * BLOCK), BF16),
            pltpu.VMEM((tbd * k, BLOCK, BLOCK), BF16),
            pltpu.VMEM((tbd, chunk, BLOCK), BF16),
            pltpu.VMEM((2, n, cap, chunk, BLOCK), BF16),
            pltpu.VMEM((n * cap, chunk, BLOCK), BF16),
            pltpu.VMEM((n * cap, chunk, BLOCK), BF16),
            pltpu.VMEM((2, 8, BLOCK), F32),
            pltpu.VMEM((2, n, 8, BLOCK), F32),
            pltpu.VMEM((BLOCK, BLOCK), F32),
            pltpu.VMEM((n, chunk, BLOCK), F32),
            pltpu.VMEM((chunk, BLOCK), F32),
            pltpu.VMEM((sbd, chunk, BLOCK), F32),
            pltpu.VMEM((nc * 8, BLOCK), F32),
            pltpu.VMEM((n, nc * 8, BLOCK), F32),
            pltpu.VMEM((8, BLOCK), F32),
            pltpu.VMEM((ndp, 8, BLOCK), F32),
            dma((3,)), dma((2, n)), dma((2, n)), dma((2, n)), dma((2, n)),
            dma((n,)), dma((n,)), dma((ndp,)), dma((ndp,)),
            pltpu.SemaphoreType.REGULAR((n,)),
        ],
        compiler_params=pltpu.CompilerParams(
            collective_id=0, has_side_effects=True, vmem_limit_bytes=64 * 2**20 - 65536),
    )(*tabs, inv, mask, teacher_logits, student_logits, weights)
    return loss[:, :chunk].reshape(rows), mean[0, 0]


def solution(mesh):
    in_specs = (P("dp", "vocab"), P("dp", "vocab"), P(), P("vocab", None, None, None), P("dp"))
    out_specs = (P("dp"), P())
    return jax.shard_map(local, mesh=mesh, in_specs=in_specs, out_specs=out_specs, check_vma=False)
```

profile of v0, /device:TPU:0, one launch (start us, length us, event | category | flops | bytes accessed | tf_op | source)
XLA Modules:
  0.0 365.4 jit_solution(16773572831088583870)
XLA Ops:
  0.6 0.0 copy-start.1
  0.6 0.7 broadcast_remainder_fusion
  1.4 0.2 copy.18
  1.6 0.2 rem.54
  1.9 0.3 copy.19
  2.1 0.2 div.38
  2.3 0.7 sign_compare_fusion
  3.1 0.3 copy.17
  3.4 0.2 ne.80
  3.7 0.5 convert_reduce_fusion.1
  4.2 0.7 select_reduce_fusion.1
  5.0 0.1 copy.20
  5.0 0.1 mul.36
  5.1 0.2 convert_reduce_fusion.2
  5.4 0.2 select_reduce_fusion
  5.5 0.6 fusion.6
  6.1 0.1 slice_compare_fusion
  6.2 0.7 subtract_select_fusion.last
  6.9 0.1 convert_reduce_fusion.3
  7.0 0.1 select_reduce_fusion.2.sidx
  7.2 0.0 copy-start
  7.2 0.6 add_select_fusion.2
  7.8 0.7 add_convert_fusion.keep
  8.5 0.6 broadcast_minimum_fusion.rblk
  9.0 0.0 copy-done
  9.0 6.3 %convert_reduce_fusion = f32[148,128]{1,0:T(8,128)S(1)} fusion(bf16[148,2,128,128]{3,2,1,0:T(8,128)(2,1)} %param.8), kind=kLoop, calls=%fused_computation | loop fusion | flops 9680384 | bytes 9775104 | tf_op jit(solution)/shard_map/reduce_sum | solution.py:292
  15.3 0.6 broadcast_divide_fusion.inv_ref
  16.0 0.0 copy-done.1
  16.0 0.1 reshape.112
  16.1 0.6 pad.4.mask_ref
  16.7 346.2 %shard_map.68 = (f32[4,128]{1,0:T(4,128)}, f32[8,128]{1,0:T(8,128)}) custom-call(s32[296]{0:T(512)} %copy-done, s32[296]{0:T(512)} %get-tuple-element.15.sblk, s32[296]{0:T(512)} %get-tuple-element.14.rord, s32[296]{0:T(512)} %broadcast_minimum_fusion.rblk, s32[296]{0:T(512)} %get-tuple-element.13.rsrc, f32[296]{0:T(512)} %add_convert_fusion.keep, ...), custom_call_target="tpu_custom_call" | custom-call | tf_op jit(solution)/shard_map/pallas_call | solution.py:299
  362.9 1.3 reshape.114
  364.2 1.2 slice.15
  (8 shorter events, 0.1 us)
Async XLA Ops:
  0.6 15.4 %copy-start.1 = (s32[384]{0:T(512)S(1)}, s32[384]{0:T(512)}, u32[]{:S(2)}) copy-start(s32[384]{0:T(512)} %param.9) | copy-start | bytes 4612
  7.2 1.8 copy-start
where the time goes:
time: 366 us; the launch traced here: 365 us
  Pallas kernels  346 us (95%)
  other arithmetic  13.6 us (4%)
  local copies, waits for them, and re-layouts  4.86 us (1%)
    pallas_call x1, Pallas kernels, local(): pl.pallas_call(functools.partial(kernel, n, ndp, cap, tbd, sbd, chunk, nc...  346 us

commit v1 on v0

v1 whole, which is shorter than its diff:
```python
import functools
import math

import jax
import jax.numpy as jnp
from jax import lax
from jax.experimental import pallas as pl
from jax.experimental.pallas import tpu as pltpu
from jax.sharding import PartitionSpec as P

BLOCK = 128
SMOOTH = 0.1
CHUNK = 64
CORES = 2
F32 = jnp.float32
BF16 = jnp.bfloat16


def kernel(n, side, ndp, cap, kk, tbd, sbd, chunk, nk, c0,
           sidx, sblk, mord, msrc, mkeep, glast, ghas,
           mask_ref, t_hbm, s_hbm, w_hbm, loss_ref, mean_ref,
           tbuf, stbuf, wbuf, prob, sbuf, rb00, rb01, rb10, rb11, pscan, pown, dsnd, drcv,
           st_send, st_recv, tr, scl, smx, ftr, fsend, frecv, dsend, drecv,
           in_sem, w_sem, rs_sem, rr_sem, ds_sem, dr_sem, sts_sem, str_sem,
           fs_sem, fr_sem, es_sem, er_sem, credit, dcredit):
    half = chunk // 2
    group = CORES * side
    count = group * cap
    me = lax.axis_index("vocab")
    my_dp = lax.axis_index("dp")
    y, x, c = me // group, (me // CORES) % side, me % CORES
    rbuf = ((rb00, rb01), (rb10, rb11))
    shape = (chunk, BLOCK)
    hshape = (half, BLOCK)
    zeros = jnp.zeros(shape, F32)
    hzeros = jnp.zeros(hshape, F32)
    lane = lax.broadcasted_iota(jnp.int32, shape, 1)
    hlane = lax.broadcasted_iota(jnp.int32, hshape, 1)
    peers = [lax.rem(me + j, n) for j in range(1, n)]
    dp_peers = [lax.rem(my_dp + j, ndp) for j in range(1, ndp)]

    def dev(yy, xx, cc):
        return (yy * side + xx) * CORES + cc

    offs = [(dy, dx, dc) for dy in range(side) for dx in range(side) for dc in range(CORES)]
    offs.sort(key=lambda o: (-((o[0] > 0) + (o[1] > 0)), o[2] if o[0] or o[1] else 1 - o[2], o[0] > 0))
    slots = {}
    for h in range(2):
        for o in offs:
            if o[1 - h] or o[2]:
                slots[h, o] = len([1 for q in slots if q[0] == h])

    def parts(h, o):
        yd, xd, cd = lax.rem(y + o[0], side), lax.rem(x + o[1], side), lax.rem(c + o[2], CORES)
        if h == 0:
            return dev(y, xd, cd), yd, xd * CORES + cd
        return dev(yd, x, cd), xd, yd * CORES + cd

    mine = (x * CORES + c, y * CORES + c)

    def place(h, g, inner):
        return pl.ds((g * side + inner) * cap, cap)

    def raw_copy(par, h, o):
        j = slots[h, o]
        peer, inner, _ = parts(h, o)
        return pltpu.make_async_remote_copy(
            src_ref=sbuf.at[par, h, j], dst_ref=rbuf[par][h].at[place(h, mine[h], inner)],
            send_sem=rs_sem.at[par, h, j], recv_sem=rr_sem.at[par, h, mine[h] * side + inner],
            device_id={"vocab": peer})

    def members(h):
        out = []
        for da in range(side):
            for dc in range(CORES):
                if da or dc:
                    a = lax.rem((y if h else x) + da, side)
                    cs = lax.rem(c + dc, CORES)
                    out.append((dev(a, x, cs) if h else dev(y, a, cs), a * CORES + cs))
        return out

    def raw_wait(par, h):
        for src, g in members(h):
            for inner in range(side):
                pltpu.make_async_remote_copy(
                    src_ref=sbuf.at[par, h, 0], dst_ref=rbuf[par][h].at[place(h, g, inner)],
                    send_sem=rs_sem.at[par, h, 0], recv_sem=rr_sem.at[par, h, g * side + inner],
                    device_id={"vocab": src}).wait_recv()

    def along(h, r):
        return dev(y, lax.rem(x + r, side), c) if h else dev(lax.rem(y + r, side), x, c)

    def dense_copy(par, h, r, back=False):
        return pltpu.make_async_remote_copy(
            src_ref=dsnd.at[par, h, r - 1], dst_ref=drcv.at[par, h, r - 1],
            send_sem=ds_sem.at[par, h, r - 1], recv_sem=dr_sem.at[par, h, r - 1],
            device_id={"vocab": along(h, side - r if back else r)})

    def stat_copy(par, k, j):
        return pltpu.make_async_remote_copy(
            src_ref=st_send.at[k], dst_ref=st_recv.at[k, me],
            send_sem=sts_sem.at[par, j], recv_sem=str_sem.at[k, me],
            device_id={"vocab": peers[j]})

    def stat_wait(k, src):
        pltpu.make_async_remote_copy(
            src_ref=st_send.at[k], dst_ref=st_recv.at[k, src],
            send_sem=sts_sem.at[0, 0], recv_sem=str_sem.at[k, src],
            device_id={"vocab": src}).wait_recv()

    def cols(b):
        return pl.ds(pl.multiple_of(b * BLOCK, BLOCK), BLOCK)

    def rows(k):
        return pl.ds(pl.multiple_of(k * chunk, chunk), chunk)

    def load_t(k):
        return pltpu.make_async_copy(t_hbm.at[rows(k)], tbuf, in_sem.at[0])

    def load_s(k):
        return pltpu.make_async_copy(s_hbm.at[rows(k)], stbuf, in_sem.at[1])

    wp = math.gcd(tbd, 4)
    wn = tbd // wp * kk

    def load_w(q):
        return pltpu.make_async_copy(w_hbm.at[pl.ds(q * wn, wn)], wbuf.at[pl.ds(q * wn, wn)], w_sem.at[q])

    def bcast(column, to=shape):
        return jnp.broadcast_to(column, to)

    load_t(0).start()
    for q in range(wp):
        load_w(q).start()
    load_s(0).start()

    barrier = pltpu.get_barrier_semaphore()
    for d in peers:
        pl.semaphore_signal(barrier, inc=1, device_id={"vocab": d})
    for e in dp_peers:
        pl.semaphore_signal(barrier, inc=1, device_id={"dp": e})
    tr[...] = jnp.zeros_like(tr)
    ftr[...] = jnp.zeros_like(ftr)
    pl.semaphore_wait(barrier, n + ndp - 2)

    def scale_weights():
        for q in range(wp):
            load_w(q).wait()

            def one(b, carry):
                tiles = [wbuf[b * kk + j].astype(F32) for j in range(kk)]
                inv = 1.0 / jnp.sum(sum(tiles), axis=1, keepdims=True)
                for j in range(kk):
                    wbuf[b * kk + j] = (tiles[j] * inv).astype(BF16)
                return carry
            lax.fori_loop(q * (tbd // wp), (q + 1) * (tbd // wp), one, 0, unroll=4)

    def produce(k, par):
        load_t(k).wait()
        tmax = lax.fori_loop(
            0, tbd, lambda b, m: jnp.maximum(m, tbuf[:, cols(b)].astype(F32)),
            jnp.full(shape, -jnp.inf, F32), unroll=4)
        tmax = bcast(jnp.max(tmax, axis=1, keepdims=True))

        def expo(b, total):
            e = jnp.exp(tbuf[:, cols(b)].astype(F32) - tmax)
            prob[b] = e.astype(BF16)
            return total + e

        total = lax.fori_loop(0, tbd, expo, zeros, unroll=4)

        @pl.when(k + 1 < nk)
        def _():
            load_t(k + 1).start()

        tsum = bcast(jnp.sum(total, axis=1, keepdims=True))
        stat = jnp.where(lane == 0, tmax, jnp.where(lane == 1, tsum, 0.0))
        stat = jnp.concatenate([stat, jnp.zeros((BLOCK - chunk, BLOCK), F32)], axis=0).T[:8]
        st_send[k] = stat
        st_recv[k, me] = stat

        @pl.when(k == 0)
        def _():
            scale_weights()

        @pl.when(k >= 2)
        def _():
            for j in range(n - 1):
                stat_copy(par, k, j).wait_send()
            for h in range(2):
                for _, g in members(h):
                    pl.semaphore_wait(credit.at[h, g], 1)
        for j in range(n - 1):
            stat_copy(par, k, j).start()

        for o in offs:
            yd, xd, cd = lax.rem(y + o[0], side), lax.rem(x + o[1], side), lax.rem(c + o[2], CORES)
            d = dev(yd, xd, cd)
            dst = []
            for h in range(2):
                if (h, o) in slots:
                    @pl.when(k >= 2)
                    def _(h=h, o=o):
                        raw_copy(par, h, o).wait_send()
                    dst.append(sbuf.at[par, h, slots[h, o]])
                else:
                    dst.append(rbuf[par][h].at[place(h, mine[h], parts(h, o)[1])])

            def one(r, carry):
                i = sidx[d * cap + r]
                b = sblk[d * cap + r]
                res = jnp.dot(prob[b], wbuf[i], preferred_element_type=F32).astype(BF16)
                dst[0][r] = res[:half]
                dst[1][r] = res[half:]
                return carry
            lax.fori_loop(0, cap, one, 0, unroll=4)
            for h in range(2):
                if (h, o) in slots:
                    raw_copy(par, h, o).start()

    def merge(k, par):
        for d in peers:
            stat_wait(k, d)
        groups = (n * 8 + BLOCK - 1) // BLOCK
        per = BLOCK // 8
        columns = []
        for g in range(groups):
            for j in range(min(per, n - g * per)):
                tr[j * 8:j * 8 + 8, :] = st_recv[k, g * per + j]
            block = tr[...].T
            for j in range(min(per, n - g * per)):
                columns.append((block[:chunk, 8 * j:8 * j + 1], block[:chunk, 8 * j + 1:8 * j + 2]))
        gmax = functools.reduce(jnp.maximum, [m for m, _ in columns])
        gsum = sum(s * jnp.exp(m - gmax) for m, s in columns)
        for j, (m, _) in enumerate(columns):
            scl[j] = bcast(jnp.exp(m - gmax) / gsum)

        def scan(h, rel, dst):
            base = (h * side + rel) * count

            def step(i, acc):
                t = rbuf[par][h][mord[base + i]].astype(F32)
                acc = acc * mkeep[base + i] + t * scl[msrc[base + i], h * half:h * half + half]
                dst[i] = acc
                return acc
            lax.fori_loop(0, count, step, hzeros, unroll=4)

        for h in range(2):
            raw_wait(par, h)
            for r in range(1, side):
                scan(h, r, pscan)

                @pl.when(k >= 2)
                def _(h=h, r=r):
                    dense_copy(par, h, r).wait_send()
                base = (h * side + r) * sbd

                def pick(s, carry):
                    dsnd[par, h, r - 1, s] = (pscan[glast[base + s]] * ghas[base + s]).astype(BF16)
                    return carry
                lax.fori_loop(0, sbd, pick, 0, unroll=4)

                @pl.when(k >= 2)
                def _(h=h, r=r):
                    pl.semaphore_wait(dcredit.at[h, r - 1], 1)
                dense_copy(par, h, r).start()
        for h in range(2):
            scan(h, 0, pown.at[par, h])

            @pl.when(k + 2 < nk)
            def _(h=h):
                for src, _ in members(h):
                    pl.semaphore_signal(credit.at[h, mine[h]], inc=1, device_id={"vocab": src})

    def consume(k, par):
        load_s(k).wait()
        m = lax.fori_loop(
            0, sbd, lambda b, m: jnp.maximum(m, stbuf[:, cols(b)].astype(F32)),
            jnp.full(shape, -jnp.inf, F32), unroll=4)
        m = bcast(jnp.max(m, axis=1, keepdims=True))
        smx[...] = m
        total = lax.fori_loop(
            0, sbd, lambda b, t: t + jnp.exp(stbuf[:, cols(b)].astype(F32) - m), zeros, unroll=4)
        ssum = jnp.sum(total, axis=1, keepdims=True)
        pieces = []
        for h in range(2):
            for r in range(1, side):
                dense_copy(par, h, r, back=True).wait_recv()
            base = h * side * sbd
            top = smx[h * half:h * half + half]

            def step(s, carry):
                tot, kla = carry
                acc = pown[par, h, glast[base + s]] * ghas[base + s]
                for r in range(1, side):
                    acc = acc + drcv[par, h, r - 1, s].astype(F32)
                tgt = (1.0 - SMOOTH) * acc + c0
                z = stbuf[h * half:h * half + half, cols(s)].astype(F32) - top
                return tot + tgt, kla + tgt * (jnp.log(tgt) - z)

            tot, kla = lax.fori_loop(0, sbd, step, (hzeros,) * 2, unroll=4)
            tot, kla = [jnp.sum(v, axis=1, keepdims=True) for v in (tot, kla)]
            pieces.append(jnp.where(
                hlane == 0, kla, jnp.where(hlane == 1, tot, jnp.where(
                    hlane == 2, top, ssum[h * half:h * half + half]))))

        @pl.when(k + 1 < nk)
        def _():
            load_s(k + 1).start()

        @pl.when(k + 2 < nk)
        def _():
            for h in range(2):
                for r in range(1, side):
                    pl.semaphore_signal(dcredit.at[h, r - 1], inc=1, device_id={"vocab": along(h, side - r)})
        per = BLOCK // chunk
        ftr[pl.ds(pl.multiple_of(lax.rem(k, per) * chunk, chunk), chunk), :] = jnp.concatenate(pieces, axis=0)
        fsend[k // per] = ftr[...].T[:8]

    def pair(j, carry):
        for par in range(2):
            it = 2 * j + par

            @pl.when(it < nk)
            def _():
                produce(it, par)

            @pl.when((it >= 1) & (it <= nk))
            def _():
                merge(it - 1, 1 - par)

            @pl.when((it >= 2) & (it <= nk + 1))
            def _():
                consume(it - 2, par)
        return carry

    lax.fori_loop(0, (nk + 3) // 2, pair, 0)

    def fin_copy(d, src):
        return pltpu.make_async_remote_copy(
            src_ref=fsend, dst_ref=frecv.at[src], send_sem=fs_sem.at[d],
            recv_sem=fr_sem.at[src], device_id={"vocab": d})

    def dp_copy(e, src):
        return pltpu.make_async_remote_copy(
            src_ref=dsend, dst_ref=drecv.at[src], send_sem=es_sem.at[e],
            recv_sem=er_sem.at[src], device_id={"dp": e})

    for d in peers:
        fin_copy(d, me).start()
    frecv[me] = fsend[...]
    for d in peers:
        fin_copy(d, d).wait_recv()
    dsend[...] = jnp.zeros_like(dsend)
    for r in range(nk * chunk // BLOCK):
        parts_ = [frecv[v, r] for v in range(n)]
        gmax = functools.reduce(jnp.maximum, [p[2:3] for p in parts_])
        lse = gmax + jnp.log(sum(p[3:4] * jnp.exp(p[2:3] - gmax) for p in parts_))
        kl = sum(p[0:1] + p[1:2] * (lse - p[2:3]) for p in parts_)
        mask = mask_ref[r:r + 1, :].astype(F32)
        loss = mask * kl
        loss_ref[r:r + 1, :] = loss
        dsend[0:1, :] += loss
        dsend[1:2, :] += mask
    for e in dp_peers:
        dp_copy(e, my_dp).start()
    drecv[my_dp] = dsend[...]
    for e in dp_peers:
        dp_copy(e, e).wait_recv()
    sums = sum(drecv[v] for v in range(ndp))
    mean_ref[...] = jnp.broadcast_to(
        jnp.sum(sums[0:1], axis=1, keepdims=True) / jnp.sum(sums[1:2], axis=1, keepdims=True),
        (8, BLOCK))
    for d in peers:
        fin_copy(d, d).wait_send()
    for e in dp_peers:
        dp_copy(e, e).wait_send()
    for k in range(max(nk - 2, 0), nk):
        for j in range(n - 1):
            stat_copy(k % 2, k, j).wait_send()
        for h, o in slots:
            raw_copy(k % 2, h, o).wait_send()
        for h in range(2):
            for r in range(1, side):
                dense_copy(k % 2, h, r).wait_send()


def tables(tile_dest, n, side, cap, tbd, sbd, me):
    i32 = jnp.int32
    kk = tile_dest.shape[1]
    per = tbd * kk
    group = CORES * side
    y, x, c = me // group, (me // CORES) % side, me % CORES
    dest = tile_dest.reshape(n, per)
    owner = dest // sbd
    block = dest % sbd
    before = jnp.arange(per)[:, None] < jnp.arange(per)[None, :]
    mine = lax.dynamic_index_in_dim(owner, me, 0, keepdims=False)
    rank = jnp.sum((mine[:, None] == mine[None, :]) & before, axis=0, dtype=i32)
    slot = mine * cap + rank
    hit = slot[:, None] == jnp.arange(n * cap)[None, :]
    sidx = jnp.sum(jnp.where(hit, jnp.arange(per, dtype=i32)[:, None], 0), axis=0)

    def sources(a):
        first = lax.dynamic_slice_in_dim(a, y * group, group, 0)
        second = lax.dynamic_index_in_dim(a.reshape(side, side, CORES, per), x, 1, keepdims=False)
        return jnp.stack([first, second.reshape(group, per)])

    owns, blks = sources(owner), sources(block)
    rel = jnp.arange(side, dtype=i32)
    inner = jnp.stack([(y + rel) % side, (x + rel) % side])
    dests = jnp.stack([(inner[0] * side + x) * CORES + c, (y * side + inner[1]) * CORES + c])
    here = owns[:, None] == dests[:, :, None, None]
    rrank = jnp.sum(here[..., :, None] & before, axis=-2, dtype=i32)
    rhit = here[..., None] & (rrank[..., None] == jnp.arange(cap))
    rb = jnp.sum(jnp.where(rhit, blks[:, None, :, :, None] + 1, 0), axis=-2)
    count = group * cap
    rb = rb.reshape(2 * side, count)
    ids = jnp.arange(count, dtype=i32)
    key = jnp.where(rb > 0, rb - 1, sbd) * count + ids
    pos = jnp.sum(key[:, None, :] < key[:, :, None], axis=2, dtype=i32)
    order = jnp.sum(jnp.where(pos[:, :, None] == ids, key[:, :, None], 0), axis=1)
    blk = order // count
    o = order % count
    g = o // cap
    inner = inner.reshape(2 * side, 1)
    mord = (g * side + inner) * cap + o % cap
    along_y = jnp.arange(2 * side)[:, None] >= side
    msrc = jnp.where(along_y, (g // CORES * side + x) * CORES + g % CORES, y * group + g)
    same = blk[:, 1:] == blk[:, :-1]
    keep = jnp.concatenate([jnp.zeros((2 * side, 1), bool), same], axis=1).astype(F32)
    s = jnp.arange(sbd)[:, None]
    upto = jnp.sum(blk[:, None, :] <= s, axis=2, dtype=i32)
    has = jnp.sum(blk[:, None, :] == s, axis=2, dtype=i32) > 0
    flat = [a.reshape(-1) for a in (mord, msrc, keep, jnp.maximum(upto - 1, 0), has.astype(F32))]
    return [sidx, sidx // kk] + flat


def local(teacher_logits, student_logits, tile_dest, tile_weight, token_mask):
    n = lax.axis_size("vocab")
    ndp = lax.axis_size("dp")
    me = lax.axis_index("vocab")
    rows = teacher_logits.shape[0]
    tbd = teacher_logits.shape[1] // BLOCK
    sbd = student_logits.shape[1] // BLOCK
    kk = tile_dest.shape[1]
    cap = (tbd * kk + n - 1) // n
    side = math.isqrt(n // CORES)
    assert side * side * CORES == n and rows % BLOCK == 0
    group = CORES * side
    chunk = CHUNK
    half = chunk // 2
    nk = rows // chunk
    c0 = SMOOTH / (sbd * BLOCK * n)
    tabs = tables(tile_dest, n, side, cap, tbd, sbd, me)
    weights = tile_weight.reshape(tbd * kk, BLOCK, BLOCK)
    smem = pl.BlockSpec(memory_space=pltpu.SMEM)
    anyspec = pl.BlockSpec(memory_space=pl.ANY)
    vmem = pl.BlockSpec(memory_space=pltpu.VMEM)
    dma = pltpu.SemaphoreType.DMA
    reg = pltpu.SemaphoreType.REGULAR
    mask = token_mask.reshape(rows // BLOCK, BLOCK)
    tiles = group * side * cap
    loss, mean = pl.pallas_call(
        functools.partial(kernel, n, side, ndp, cap, kk, tbd, sbd, chunk, nk, c0),
        out_shape=[jax.ShapeDtypeStruct((rows // BLOCK, BLOCK), F32), jax.ShapeDtypeStruct((8, BLOCK), F32)],
        in_specs=[smem] * 7 + [vmem] + [anyspec] * 3,
        out_specs=[vmem] * 2,
        scratch_shapes=[
            pltpu.VMEM((chunk, tbd * BLOCK), BF16),
            pltpu.VMEM((chunk, sbd * BLOCK), BF16),
            pltpu.VMEM((tbd * kk, BLOCK, BLOCK), BF16),
            pltpu.VMEM((tbd, chunk, BLOCK), BF16),
            pltpu.VMEM((2, 2, n - side, cap, half, BLOCK), BF16)]
            + [pltpu.VMEM((tiles, half, BLOCK), BF16)] * 4 + [
            pltpu.VMEM((group * cap, half, BLOCK), F32),
            pltpu.VMEM((2, 2, group * cap, half, BLOCK), F32),
            pltpu.VMEM((2, 2, side - 1, sbd, half, BLOCK), BF16),
            pltpu.VMEM((2, 2, side - 1, sbd, half, BLOCK), BF16),
            pltpu.VMEM((nk, 8, BLOCK), F32),
            pltpu.VMEM((nk, n, 8, BLOCK), F32),
            pltpu.VMEM((BLOCK, BLOCK), F32),
            pltpu.VMEM((n, chunk, BLOCK), F32),
            pltpu.VMEM((chunk, BLOCK), F32),
            pltpu.VMEM((BLOCK, BLOCK), F32),
            pltpu.VMEM((rows // BLOCK, 8, BLOCK), F32),
            pltpu.VMEM((n, rows // BLOCK, 8, BLOCK), F32),
            pltpu.VMEM((8, BLOCK), F32),
            pltpu.VMEM((ndp, 8, BLOCK), F32),
            dma((2,)), dma((4,)),
            dma((2, 2, n - side)), dma((2, 2, group * side)),
            dma((2, 2, side - 1)), dma((2, 2, side - 1)),
            dma((2, n - 1)), dma((nk, n)),
            dma((n,)), dma((n,)), dma((ndp,)), dma((ndp,)),
            reg((2, group)), reg((2, side - 1)),
        ],
        compiler_params=pltpu.CompilerParams(
            collective_id=0, has_side_effects=True, vmem_limit_bytes=64 * 2**20 - 65536),
    )(*tabs, mask, teacher_logits, student_logits, weights)
    return loss.reshape(rows), mean[0, 0]


def solution(mesh):
    in_specs = (P("dp", "vocab"), P("dp", "vocab"), P(), P("vocab", None, None, None), P("dp"))
    out_specs = (P("dp"), P())
    return jax.shard_map(local, mesh=mesh, in_specs=in_specs, out_specs=out_specs, check_vma=False)
```

time: 366 us -> 338 us (0.923)
  Pallas kernels: 346 us -> 319 us
    pallas_call x1, Pallas kernels: 346 us -> 319 us  [local(): pl.pallas_call(functools.partial(kernel, n, side, ndp, cap, kk, tbd, sbd,...]
where the time goes in v1:
time: 338 us
  Pallas kernels  319 us (94%)
  other arithmetic  10.5 us (3%)
  local copies, waits for them, and re-layouts  7.9 us (2%)
    pallas_call x1, Pallas kernels, local(): pl.pallas_call(functools.partial(kernel, n, side, ndp, cap, kk, tbd, sbd,...  319 us

profile of v1, /device:TPU:0, one launch (start us, length us, event | category | flops | bytes accessed | tf_op | source)
XLA Modules:
  0.0 338.1 jit_solution(11227452637630330056)
XLA Ops:
  0.7 0.1 broadcast_in_dim.48
  0.8 0.1 broadcast_in_dim.49
  0.9 0.1 add.283
  1.0 0.1 add.284
  1.1 0.1 add.285
  1.2 0.7 sign_compare_fusion
  1.9 0.7 broadcast_remainder_fusion
  2.7 0.3 copy.30
  3.0 0.2 ne.197
  3.2 0.4 ne.205
  3.6 0.2 copy.31
  3.8 0.3 rem.177
  4.2 0.2 rem.165
  4.4 0.2 copy.32
  4.7 0.3 div.70
  5.0 0.2 div.63
  5.3 0.1 convert_reduce_fusion.2
  5.5 0.1 select_reduce_fusion.2.sidx
  5.6 0.0 copy-start
  5.6 0.6 add_select_fusion.8.sblk
  6.2 0.1 broadcast_compare_fusion
  6.3 1.0 convert_reduce_fusion
  7.3 0.0 copy-done
  7.3 2.6 select_reduce_fusion
  9.9 0.1 copy.36
  10.0 0.1 mul.91
  10.1 0.1 copy.38
  10.2 2.7 convert_reduce_fusion.1
  13.0 0.6 select_reduce_fusion.1
  13.6 0.1 rem.205
  13.7 0.6 fusion.8
  14.3 0.1 slice_compare_fusion
  14.4 0.1 pad_convert_fusion
  14.4 0.7 reshape.273.mkeep
  15.1 0.1 copy.39
  15.2 0.3 convert_reduce_fusion.3
  15.5 0.7 reshape.274.ghas
  16.2 0.7 max.8.glast
  16.9 318.8 %shard_map.68 = (f32[3,128]{1,0:T(4,128)}, f32[8,128]{1,0:T(8,128)}) custom-call(s32[296]{0:T(512)} %copy-done, s32[296]{0:T(512)} %add_select_fusion.8.sblk, s32[592]{0:T(1024)} %get-tuple-element.17.mord, s32[592]{0:T(1024)} %get-tuple-element.16.msrc, f32[592]{0:T(1024)} %reshape.273.mkeep, s32[496]{0:T(512)} %max.8.glast, f32[496]{0:T(512)} %reshape.274.ghas, ...), custom_call_target="tpu_custom_call" | custom-call | tf_op jit(solution)/shard_map/pallas_call | solution.py:464
  335.6 1.2 slice.11
  336.8 1.3 copy.41
  (21 shorter events, 0.3 us)
Async XLA Ops:
  5.6 1.7 copy-start

commit v2 on v1

--- a/solution.py
+++ b/solution.py
@@ -16,11 +16,82 @@
 BF16 = jnp.bfloat16
 
 
+def build_tables(n, side, cap, kk, tbd, sbd, y, x, c, me, dest_ref, itab, ftab):
+    group = CORES * side
+    count = group * cap
+    i32 = jnp.int32
+
+    def iota(shape, dim):
+        return lax.broadcasted_iota(i32, shape, dim)
+
+    def add(mask, value, axis):
+        return jnp.sum(jnp.where(mask, value, 0), axis=axis, keepdims=True, dtype=i32)
+
+    def column(row):
+        size = row.shape[1]
+        square = (size, size)
+        return add(iota(square, 0) == iota(square, 1), jnp.broadcast_to(row, square), 1)
+
+    earlier = iota((tbd, tbd), 1) < iota((tbd, tbd), 0)
+
+    def source(v):
+        rows = [dest_ref[j, pl.ds(v, 1), :] for j in range(kk)]
+        owns = [sum(jnp.where(row >= d * sbd, 1, 0) for d in range(1, n)) for row in rows]
+        cols = [column(own) for own in owns]
+        found = []
+        for j, owner in enumerate(cols):
+            same = [own == owner for own in owns[:j + 1]]
+            same[j] = same[j] & earlier
+            rank = jnp.sum(sum(jnp.where(m, 1, 0) for m in same), axis=1, keepdims=True, dtype=i32)
+            found.append((owner, column(rows[j]) - owner * sbd, rank))
+        return found
+
+    def put(ref, r, row):
+        ref[r:r + 1, :row.shape[1]] = row
+
+    sblk = jnp.zeros((1, n * cap), i32)
+    sidx = jnp.zeros((1, n * cap), i32)
+    for j, (owner, _, rank) in enumerate(source(me)):
+        hit = owner * cap + rank == iota((tbd, n * cap), 1)
+        sblk = sblk + add(hit, iota((tbd, n * cap), 0), 0)
+        sidx = sidx + add(hit, iota((tbd, n * cap), 0) * kk + j, 0)
+    put(itab, 0, sidx)
+    put(itab, 1, sblk)
+    square = (count, count)
+    before = iota(square, 1) < iota(square, 0)
+    slot = iota((count, 1), 0)
+    member = sum(jnp.where(slot >= g * cap, 1, 0) for g in range(1, group))
+    for h in range(2):
+        devs = [(g // CORES * side + x) * CORES + g % CORES if h else y * group + g for g in range(group)]
+        found = [source(v) for v in devs]
+        from_dev = sum(jnp.where(member == g, v, 0) for g, v in enumerate(devs))
+        for rel in range(side):
+            inner = lax.rem((x if h else y) + rel, side)
+            d = (y * side + inner if h else inner * side + x) * CORES + c
+            rb = jnp.zeros((1, count), i32)
+            for g, tiles in enumerate(found):
+                for owner, block, rank in tiles:
+                    at = jnp.where(owner == d, rank + g * cap, -1)
+                    rb = rb + add(at == iota((tbd, count), 1), block + 1, 0)
+            row = jnp.where(rb > 0, rb - 1, sbd)
+            col = column(row)
+            again = jnp.where((row == col) & before, 1, 0)
+            cont = jnp.sum(again, axis=1, keepdims=True, dtype=i32)
+            pos = jnp.sum(again + jnp.where(row < col, 1, 0), axis=1, keepdims=True, dtype=i32)
+            place = pos == iota(square, 1)
+            base = h * side + rel
+            put(itab, 2 + 3 * base, add(place, slot + member * ((side - 1) * cap) + inner * cap, 0))
+            put(itab, 3 + 3 * base, add(place, from_dev, 0))
+            s = iota((count, sbd), 1)
+            put(itab, 4 + 3 * base, jnp.maximum(add(col <= s, 1, 0) - 1, 0))
+            put(ftab, 2 * base, jnp.where(add(place, cont, 0) > 0, 1.0, 0.0))
+            put(ftab, 2 * base + 1, jnp.where(add(col == s, 1, 0) > 0, 1.0, 0.0))
+
+
 def kernel(n, side, ndp, cap, kk, tbd, sbd, chunk, nk, c0,
-           sidx, sblk, mord, msrc, mkeep, glast, ghas,
-           mask_ref, t_hbm, s_hbm, w_hbm, loss_ref, mean_ref,
-           tbuf, stbuf, wbuf, prob, sbuf, rb00, rb01, rb10, rb11, pscan, pown, dsnd, drcv,
-           st_send, st_recv, tr, scl, smx, ftr, fsend, frecv, dsend, drecv,
+           dest_ref, mask_ref, t_hbm, s_hbm, w_hbm, loss_ref, mean_ref,
+           itab, ftab, ivec, fvec, tbuf, stbuf, wbuf, prob, sbuf, rb00, rb01, rb10, rb11, pscan, pown, dsnd, drcv,
+           st_send, st_recv, tr, scl, smx, tot, inv, ftr, fsend, frecv, dsend, drecv,
            in_sem, w_sem, rs_sem, rr_sem, ds_sem, dr_sem, sts_sem, str_sem,
            fs_sem, fr_sem, es_sem, er_sem, credit, dcredit):
     half = chunk // 2
@@ -90,10 +161,14 @@
     def along(h, r):
         return dev(y, lax.rem(x + r, side), c) if h else dev(lax.rem(y + r, side), x, c)
 
-    def dense_copy(par, h, r, back=False):
+    npc = math.gcd(sbd, 4)
+    piece = sbd // npc
+
+    def dense_copy(par, h, r, q, back=False):
+        at = pl.ds(q * piece, piece)
         return pltpu.make_async_remote_copy(
-            src_ref=dsnd.at[par, h, r - 1], dst_ref=drcv.at[par, h, r - 1],
-            send_sem=ds_sem.at[par, h, r - 1], recv_sem=dr_sem.at[par, h, r - 1],
+            src_ref=dsnd.at[par, h, r - 1, at], dst_ref=drcv.at[par, h, r - 1, at],
+            send_sem=ds_sem.at[par, h, r - 1, q], recv_sem=dr_sem.at[par, h, r - 1, q],
             device_id={"vocab": along(h, side - r if back else r)})
 
     def stat_copy(par, k, j):
@@ -120,11 +195,13 @@
     def load_s(k):
         return pltpu.make_async_copy(s_hbm.at[rows(k)], stbuf, in_sem.at[1])
 
-    wp = math.gcd(tbd, 4)
-    wn = tbd // wp * kk
+    batch = math.gcd(tbd, 4)
+    wp = min(4, tbd // batch)
+    edges = [tbd // batch * q // wp for q in range(wp + 1)]
 
     def load_w(q):
-        return pltpu.make_async_copy(w_hbm.at[pl.ds(q * wn, wn)], wbuf.at[pl.ds(q * wn, wn)], w_sem.at[q])
+        at = pl.ds(edges[q] * batch * kk, (edges[q + 1] - edges[q]) * batch * kk)
+        return pltpu.make_async_copy(w_hbm.at[at], wbuf.at[at], w_sem.at[q])
 
     def bcast(column, to=shape):
         return jnp.broadcast_to(column, to)
@@ -132,7 +209,6 @@
     load_t(0).start()
     for q in range(wp):
         load_w(q).start()
-    load_s(0).start()
 
     barrier = pltpu.get_barrier_semaphore()
     for d in peers:
@@ -141,22 +217,17 @@
         pl.semaphore_signal(barrier, inc=1, device_id={"dp": e})
     tr[...] = jnp.zeros_like(tr)
     ftr[...] = jnp.zeros_like(ftr)
+    ivec[...] = jnp.zeros_like(ivec)
+    fvec[...] = jnp.zeros_like(fvec)
+    build_tables(n, side, cap, kk, tbd, sbd, y, x, c, me, dest_ref, ivec, fvec)
+    to_smem = [pltpu.make_async_copy(ivec, itab, in_sem.at[2]), pltpu.make_async_copy(fvec, ftab, in_sem.at[3])]
+    for copy in to_smem:
+        copy.start()
     pl.semaphore_wait(barrier, n + ndp - 2)
-
-    def scale_weights():
-        for q in range(wp):
-            load_w(q).wait()
-
-            def one(b, carry):
-                tiles = [wbuf[b * kk + j].astype(F32) for j in range(kk)]
-                inv = 1.0 / jnp.sum(sum(tiles), axis=1, keepdims=True)
-                for j in range(kk):
-                    wbuf[b * kk + j] = (tiles[j] * inv).astype(BF16)
-                return carry
-            lax.fori_loop(q * (tbd // wp), (q + 1) * (tbd // wp), one, 0, unroll=4)
 
     def produce(k, par):
         load_t(k).wait()
+
         tmax = lax.fori_loop(
             0, tbd, lambda b, m: jnp.maximum(m, tbuf[:, cols(b)].astype(F32)),
             jnp.full(shape, -jnp.inf, F32), unroll=4)
@@ -164,24 +235,49 @@
 
         def expo(b, total):
             e = jnp.exp(tbuf[:, cols(b)].astype(F32) - tmax)
-            prob[b] = e.astype(BF16)
+            prob[b] = (e * inv[pl.ds(b, 1), :]).astype(BF16)
             return total + e
 
-        total = lax.fori_loop(0, tbd, expo, zeros, unroll=4)
+        @pl.when(k == 0)
+        def _():
+            ones = jnp.ones((kk * BLOCK, BLOCK), BF16)
+            square = (BLOCK, BLOCK)
+            diag = lax.broadcasted_iota(jnp.int32, square, 0) == lax.broadcasted_iota(jnp.int32, square, 1)
+
+            def both(p, total):
+                blocks = [p * batch + j for j in range(batch)]
+                wide = jnp.concatenate([
+                    jnp.concatenate([wbuf[b * kk + j] for j in range(kk)], axis=1) for b in blocks], axis=0)
+                sums = jnp.dot(wide, ones, preferred_element_type=F32)
+                for j, b in enumerate(blocks):
+                    own = jnp.where(diag, sums[j * BLOCK:(j + 1) * BLOCK], 0.0)
+                    inv[pl.ds(b, 1), :] = 1.0 / jnp.sum(own, axis=0, keepdims=True)
+                for b in blocks:
+                    total = expo(b, total)
+                return total
+
+            total = zeros
+            for q in range(wp):
+                load_w(q).wait()
+                total = lax.fori_loop(edges[q], edges[q + 1], both, total)
+            tot[...] = total
+            load_s(0).start()
+            for copy in to_smem:
+                copy.wait()
+
+        @pl.when(k > 0)
+        def _():
+            tot[...] = lax.fori_loop(0, tbd, expo, zeros, unroll=4)
 
         @pl.when(k + 1 < nk)
         def _():
             load_t(k + 1).start()
 
-        tsum = bcast(jnp.sum(total, axis=1, keepdims=True))
+        tsum = bcast(jnp.sum(tot[...], axis=1, keepdims=True))
         stat = jnp.where(lane == 0, tmax, jnp.where(lane == 1, tsum, 0.0))
         stat = jnp.concatenate([stat, jnp.zeros((BLOCK - chunk, BLOCK), F32)], axis=0).T[:8]
         st_send[k] = stat
         st_recv[k, me] = stat
-
-        @pl.when(k == 0)
-        def _():
-            scale_weights()
 
         @pl.when(k >= 2)
         def _():
@@ -206,14 +302,20 @@
                 else:
                     dst.append(rbuf[par][h].at[place(h, mine[h], parts(h, o)[1])])
 
-            def one(r, carry):
-                i = sidx[d * cap + r]
-                b = sblk[d * cap + r]
+            def one(r):
+                i = itab[0, d * cap + r]
+                b = itab[1, d * cap + r]
                 res = jnp.dot(prob[b], wbuf[i], preferred_element_type=F32).astype(BF16)
                 dst[0][r] = res[:half]
                 dst[1][r] = res[half:]
+
+            def several(q, carry):
+                for j in range(4):
+                    one(q * 4 + j)
                 return carry
-            lax.fori_loop(0, cap, one, 0, unroll=4)
+            lax.fori_loop(0, cap // 4, several, 0)
+            for r in range(cap // 4 * 4, cap):
+                one(r)
             for h in range(2):
                 if (h, o) in slots:
                     raw_copy(par, h, o).start()
@@ -236,11 +338,12 @@
             scl[j] = bcast(jnp.exp(m - gmax) / gsum)
 
         def scan(h, rel, dst):
-            base = (h * side + rel) * count
+            base = 2 + 3 * (h * side + rel)
+            fbase = 2 * (h * side + rel)
 
             def step(i, acc):
-                t = rbuf[par][h][mord[base + i]].astype(F32)
-                acc = acc * mkeep[base + i] + t * scl[msrc[base + i], h * half:h * half + half]
+                t = rbuf[par][h][itab[base, i]].astype(F32)
+                acc = acc * ftab[fbase, i] + t * scl[itab[base + 1, i], h * half:h * half + half]
                 dst[i] = acc
                 return acc
             lax.fori_loop(0, count, step, hzeros, unroll=4)
@@ -252,18 +355,17 @@
 
                 @pl.when(k >= 2)
                 def _(h=h, r=r):
-                    dense_copy(par, h, r).wait_send()
-                base = (h * side + r) * sbd
+                    for q in range(npc):
+                        dense_copy(par, h, r, q).wait_send()
+                    pl.semaphore_wait(dcredit.at[h, r - 1], 1)
+                base = h * side + r
 
                 def pick(s, carry):
-                    dsnd[par, h, r - 1, s] = (pscan[glast[base + s]] * ghas[base + s]).astype(BF16)
+                    dsnd[par, h, r - 1, s] = (pscan[itab[4 + 3 * base, s]] * ftab[2 * base + 1, s]).astype(BF16)
                     return carry
-                lax.fori_loop(0, sbd, pick, 0, unroll=4)
-
-                @pl.when(k >= 2)
-                def _(h=h, r=r):
-                    pl.semaphore_wait(dcredit.at[h, r - 1], 1)
-                dense_copy(par, h, r).start()
+                for q in range(npc):
+                    lax.fori_loop(q * piece, (q + 1) * piece, pick, 0, unroll=4)
+                    dense_copy(par, h, r, q).start()
         for h in range(2):
             scan(h, 0, pown.at[par, h])
 
@@ -282,27 +384,31 @@
         total = lax.fori_loop(
             0, sbd, lambda b, t: t + jnp.exp(stbuf[:, cols(b)].astype(F32) - m), zeros, unroll=4)
         ssum = jnp.sum(total, axis=1, keepdims=True)
+        sums = [hzeros] * 4
+        for q in range(npc):
+            for h in range(2):
+                for r in range(1, side):
+                    dense_copy(par, h, r, q, back=True).wait_recv()
+                base = h * side
+                top = smx[h * half:h * half + half]
+
+                def step(s, carry):
+                    tot, kla = carry
+                    acc = pown[par, h, itab[4 + 3 * base, s]] * ftab[2 * base + 1, s]
+                    for r in range(1, side):
+                        acc = acc + drcv[par, h, r - 1, s].astype(F32)
+                    tgt = (1.0 - SMOOTH) * acc + c0
+                    z = stbuf[h * half:h * half + half, cols(s)].astype(F32) - top
+                    return tot + tgt, kla + tgt * (jnp.log(tgt) - z)
+
+                sums[2 * h:2 * h + 2] = lax.fori_loop(
+                    q * piece, (q + 1) * piece, step, tuple(sums[2 * h:2 * h + 2]), unroll=4)
         pieces = []
         for h in range(2):
-            for r in range(1, side):
-                dense_copy(par, h, r, back=True).wait_recv()
-            base = h * side * sbd
-            top = smx[h * half:h * half + half]
-
-            def step(s, carry):
-                tot, kla = carry
-                acc = pown[par, h, glast[base + s]] * ghas[base + s]
-                for r in range(1, side):
-                    acc = acc + drcv[par, h, r - 1, s].astype(F32)
-                tgt = (1.0 - SMOOTH) * acc + c0
-                z = stbuf[h * half:h * half + half, cols(s)].astype(F32) - top
-                return tot + tgt, kla + tgt * (jnp.log(tgt) - z)
-
-            tot, kla = lax.fori_loop(0, sbd, step, (hzeros,) * 2, unroll=4)
-            tot, kla = [jnp.sum(v, axis=1, keepdims=True) for v in (tot, kla)]
+            mass, kla = [jnp.sum(v, axis=1, keepdims=True) for v in sums[2 * h:2 * h + 2]]
             pieces.append(jnp.where(
-                hlane == 0, kla, jnp.where(hlane == 1, tot, jnp.where(
-                    hlane == 2, top, ssum[h * half:h * half + half]))))
+                hlane == 0, kla, jnp.where(hlane == 1, mass, jnp.where(
+                    hlane == 2, smx[h * half:h * half + half], ssum[h * half:h * half + half]))))
 
         @pl.when(k + 1 < nk)
         def _():
@@ -325,16 +431,16 @@
             def _():
                 produce(it, par)
 
+            @pl.when((it >= 3) & (it <= nk + 2))
+            def _():
+                consume(it - 3, 1 - par)
+
             @pl.when((it >= 1) & (it <= nk))
             def _():
                 merge(it - 1, 1 - par)
-
-            @pl.when((it >= 2) & (it <= nk + 1))
-            def _():
-                consume(it - 2, par)
         return carry
 
-    lax.fori_loop(0, (nk + 3) // 2, pair, 0)
+    lax.fori_loop(0, (nk + 4) // 2, pair, 0)
 
     def fin_copy(d, src):
         return pltpu.make_async_remote_copy(
@@ -382,64 +488,13 @@
             raw_copy(k % 2, h, o).wait_send()
         for h in range(2):
             for r in range(1, side):
-                dense_copy(k % 2, h, r).wait_send()
-
-
-def tables(tile_dest, n, side, cap, tbd, sbd, me):
-    i32 = jnp.int32
-    kk = tile_dest.shape[1]
-    per = tbd * kk
-    group = CORES * side
-    y, x, c = me // group, (me // CORES) % side, me % CORES
-    dest = tile_dest.reshape(n, per)
-    owner = dest // sbd
-    block = dest % sbd
-    before = jnp.arange(per)[:, None] < jnp.arange(per)[None, :]
-    mine = lax.dynamic_index_in_dim(owner, me, 0, keepdims=False)
-    rank = jnp.sum((mine[:, None] == mine[None, :]) & before, axis=0, dtype=i32)
-    slot = mine * cap + rank
-    hit = slot[:, None] == jnp.arange(n * cap)[None, :]
-    sidx = jnp.sum(jnp.where(hit, jnp.arange(per, dtype=i32)[:, None], 0), axis=0)
-
-    def sources(a):
-        first = lax.dynamic_slice_in_dim(a, y * group, group, 0)
-        second = lax.dynamic_index_in_dim(a.reshape(side, side, CORES, per), x, 1, keepdims=False)
-        return jnp.stack([first, second.reshape(group, per)])
-
-    owns, blks = sources(owner), sources(block)
-    rel = jnp.arange(side, dtype=i32)
-    inner = jnp.stack([(y + rel) % side, (x + rel) % side])
-    dests = jnp.stack([(inner[0] * side + x) * CORES + c, (y * side + inner[1]) * CORES + c])
-    here = owns[:, None] == dests[:, :, None, None]
-    rrank = jnp.sum(here[..., :, None] & before, axis=-2, dtype=i32)
-    rhit = here[..., None] & (rrank[..., None] == jnp.arange(cap))
-    rb = jnp.sum(jnp.where(rhit, blks[:, None, :, :, None] + 1, 0), axis=-2)
-    count = group * cap
-    rb = rb.reshape(2 * side, count)
-    ids = jnp.arange(count, dtype=i32)
-    key = jnp.where(rb > 0, rb - 1, sbd) * count + ids
-    pos = jnp.sum(key[:, None, :] < key[:, :, None], axis=2, dtype=i32)
-    order = jnp.sum(jnp.where(pos[:, :, None] == ids, key[:, :, None], 0), axis=1)
-    blk = order // count
-    o = order % count
-    g = o // cap
-    inner = inner.reshape(2 * side, 1)
-    mord = (g * side + inner) * cap + o % cap
-    along_y = jnp.arange(2 * side)[:, None] >= side
-    msrc = jnp.where(along_y, (g // CORES * side + x) * CORES + g % CORES, y * group + g)
-    same = blk[:, 1:] == blk[:, :-1]
-    keep = jnp.concatenate([jnp.zeros((2 * side, 1), bool), same], axis=1).astype(F32)
-    s = jnp.arange(sbd)[:, None]
-    upto = jnp.sum(blk[:, None, :] <= s, axis=2, dtype=i32)
-    has = jnp.sum(blk[:, None, :] == s, axis=2, dtype=i32) > 0
-    flat = [a.reshape(-1) for a in (mord, msrc, keep, jnp.maximum(upto - 1, 0), has.astype(F32))]
-    return [sidx, sidx // kk] + flat
+                for q in range(npc):
+                    dense_copy(k % 2, h, r, q).wait_send()
 
 
 def local(teacher_logits, student_logits, tile_dest, tile_weight, token_mask):
     n = lax.axis_size("vocab")
     ndp = lax.axis_size("dp")
-    me = lax.axis_index("vocab")
     rows = teacher_logits.shape[0]
     tbd = teacher_logits.shape[1] // BLOCK
     sbd = student_logits.shape[1] // BLOCK
@@ -452,9 +507,10 @@
     half = chunk // 2
     nk = rows // chunk
     c0 = SMOOTH / (sbd * BLOCK * n)
-    tabs = tables(tile_dest, n, side, cap, tbd, sbd, me)
+    width = -(-max(n * cap, sbd) // BLOCK) * BLOCK
+    itab, ftab = (2 + 6 * side, width), (4 * side, width)
+    dest = tile_dest.T.reshape(kk, n, tbd)
     weights = tile_weight.reshape(tbd * kk, BLOCK, BLOCK)
-    smem = pl.BlockSpec(memory_space=pltpu.SMEM)
     anyspec = pl.BlockSpec(memory_space=pl.ANY)
     vmem = pl.BlockSpec(memory_space=pltpu.VMEM)
     dma = pltpu.SemaphoreType.DMA
@@ -464,9 +520,11 @@
     loss, mean = pl.pallas_call(
         functools.partial(kernel, n, side, ndp, cap, kk, tbd, sbd, chunk, nk, c0),
         out_shape=[jax.ShapeDtypeStruct((rows // BLOCK, BLOCK), F32), jax.ShapeDtypeStruct((8, BLOCK), F32)],
-        in_specs=[smem] * 7 + [vmem] + [anyspec] * 3,
+        in_specs=[vmem] * 2 + [anyspec] * 3,
         out_specs=[vmem] * 2,
         scratch_shapes=[
+            pltpu.SMEM(itab, jnp.int32), pltpu.SMEM(ftab, F32),
+            pltpu.VMEM(itab, jnp.int32), pltpu.VMEM(ftab, F32),
             pltpu.VMEM((chunk, tbd * BLOCK), BF16),
             pltpu.VMEM((chunk, sbd * BLOCK), BF16),
             pltpu.VMEM((tbd * kk, BLOCK, BLOCK), BF16),
@@ -482,21 +540,23 @@
             pltpu.VMEM((BLOCK, BLOCK), F32),
             pltpu.VMEM((n, chunk, BLOCK), F32),
             pltpu.VMEM((chunk, BLOCK), F32),
+            pltpu.VMEM((chunk, BLOCK), F32),
+            pltpu.VMEM((tbd, BLOCK), F32),
             pltpu.VMEM((BLOCK, BLOCK), F32),
             pltpu.VMEM((rows // BLOCK, 8, BLOCK), F32),
             pltpu.VMEM((n, rows // BLOCK, 8, BLOCK), F32),
             pltpu.VMEM((8, BLOCK), F32),
             pltpu.VMEM((ndp, 8, BLOCK), F32),
-            dma((2,)), dma((4,)),
+            dma((4,)), dma((4,)),
             dma((2, 2, n - side)), dma((2, 2, group * side)),
-            dma((2, 2, side - 1)), dma((2, 2, side - 1)),
+            dma((2, 2, side - 1, 4)), dma((2, 2, side - 1, 4)),
             dma((2, n - 1)), dma((nk, n)),
             dma((n,)), dma((n,)), dma((ndp,)), dma((ndp,)),
             reg((2, group)), reg((2, side - 1)),
         ],
         compiler_params=pltpu.CompilerParams(
             collective_id=0, has_side_effects=True, vmem_limit_bytes=64 * 2**20 - 65536),
-    )(*tabs, mask, teacher_logits, student_logits, weights)
+    )(dest, mask, teacher_logits, student_logits, weights)
     return loss.reshape(rows), mean[0, 0]
 
 

time: 338 us -> 325 us (0.962)
  other arithmetic: 10.5 us -> 0 us
  local copies, waits for them, and re-layouts: 7.9 us -> 3.82 us
    reduce_sum x7 -> x0, other arithmetic: 7.45 us -> none  [the longest x1 2.75 us: tables(): pos = jnp.sum(key[:, None, :] < key[:, :, None], axis=2, dtype=i32)]
where the time goes in v2:
time: 325 us
  Pallas kernels  320 us (98%)
  local copies, waits for them, and re-layouts  3.82 us (1%)
    pallas_call x1, Pallas kernels, local(): pl.pallas_call(functools.partial(kernel, n, side, ndp, cap, kk, tbd, sbd,...  320 us

profile of v2, /device:TPU:0, one launch (start us, length us, event | category | flops | bytes accessed | tf_op | source)
XLA Modules:
  0.0 324.6 jit_solution(15784540785465992662)
XLA Ops:
  0.6 1.4 reshape.16.dest_ref
  2.0 320.2 %shard_map.68 = (f32[3,128]{1,0:T(4,128)}, f32[8,128]{1,0:T(8,128)}) custom-call(s32[2,8,148]{2,1,0:T(8,128)} %reshape.16.dest_ref, s32[3,128]{1,0:T(4,128)} %bitcast.7, bf16[384,18944]{1,0:T(8,128)(2,1)} %t_hbm.1, bf16[384,15872]{1,0:T(8,128)(2,1)} %s_hbm.1, bf16[296,128,128]{2,1,0:T(8,128)(2,1)} %bitcast.5), custom_call_target="tpu_custom_call" | custom-call | tf_op jit(solution)/shard_map/pallas_call | solution.py:520
  322.2 1.2 slice.3
  323.4 1.2 copy.8

commit v3 on v2

--- a/solution.py
+++ b/solution.py
@@ -16,9 +16,7 @@
 BF16 = jnp.bfloat16
 
 
-def build_tables(n, side, cap, kk, tbd, sbd, y, x, c, me, dest_ref, itab, ftab):
-    group = CORES * side
-    count = group * cap
+def table_tools(n, kk, tbd, sbd, dest_ref):
     i32 = jnp.int32
 
     def iota(shape, dim):
@@ -35,28 +33,45 @@
     earlier = iota((tbd, tbd), 1) < iota((tbd, tbd), 0)
 
     def source(v):
-        rows = [dest_ref[j, pl.ds(v, 1), :] for j in range(kk)]
+        wide = (tbd, dest_ref.shape[1])
+        here = iota(wide, 1) == iota(wide, 0) + v * tbd
+        dests = [add(here, jnp.broadcast_to(dest_ref[j:j + 1, :], wide), 1) for j in range(kk)]
+        diag = iota((tbd, tbd), 0) == iota((tbd, tbd), 1)
+        rows = [add(diag, jnp.broadcast_to(d, (tbd, tbd)), 0) for d in dests]
         owns = [sum(jnp.where(row >= d * sbd, 1, 0) for d in range(1, n)) for row in rows]
-        cols = [column(own) for own in owns]
+        cols = [sum(jnp.where(d >= e * sbd, 1, 0) for e in range(1, n)) for d in dests]
         found = []
         for j, owner in enumerate(cols):
             same = [own == owner for own in owns[:j + 1]]
             same[j] = same[j] & earlier
             rank = jnp.sum(sum(jnp.where(m, 1, 0) for m in same), axis=1, keepdims=True, dtype=i32)
-            found.append((owner, column(rows[j]) - owner * sbd, rank))
+            found.append((owner, dests[j] - owner * sbd, rank))
         return found
 
     def put(ref, r, row):
         ref[r:r + 1, :row.shape[1]] = row
 
+    return iota, add, column, source, put
+
+
+def send_table(n, cap, kk, tbd, sbd, me, dest_ref, stab):
+    i32 = jnp.int32
+    iota, add, column, source, put = table_tools(n, kk, tbd, sbd, dest_ref)
     sblk = jnp.zeros((1, n * cap), i32)
     sidx = jnp.zeros((1, n * cap), i32)
     for j, (owner, _, rank) in enumerate(source(me)):
         hit = owner * cap + rank == iota((tbd, n * cap), 1)
         sblk = sblk + add(hit, iota((tbd, n * cap), 0), 0)
         sidx = sidx + add(hit, iota((tbd, n * cap), 0) * kk + j, 0)
-    put(itab, 0, sidx)
-    put(itab, 1, sblk)
+    put(stab, 0, sidx)
+    put(stab, 1, sblk)
+
+
+def receive_tables(n, side, cap, kk, tbd, sbd, y, x, c, dest_ref, itab, ftab):
+    i32 = jnp.int32
+    group = CORES * side
+    count = group * cap
+    iota, add, column, source, put = table_tools(n, kk, tbd, sbd, dest_ref)
     square = (count, count)
     before = iota(square, 1) < iota(square, 0)
     slot = iota((count, 1), 0)
@@ -80,18 +95,18 @@
             pos = jnp.sum(again + jnp.where(row < col, 1, 0), axis=1, keepdims=True, dtype=i32)
             place = pos == iota(square, 1)
             base = h * side + rel
-            put(itab, 2 + 3 * base, add(place, slot + member * ((side - 1) * cap) + inner * cap, 0))
-            put(itab, 3 + 3 * base, add(place, from_dev, 0))
+            put(itab, 3 * base, add(place, slot + member * ((side - 1) * cap) + inner * cap, 0))
+            put(itab, 1 + 3 * base, add(place, from_dev, 0))
             s = iota((count, sbd), 1)
-            put(itab, 4 + 3 * base, jnp.maximum(add(col <= s, 1, 0) - 1, 0))
+            put(itab, 2 + 3 * base, jnp.maximum(add(col <= s, 1, 0) - 1, 0))
             put(ftab, 2 * base, jnp.where(add(place, cont, 0) > 0, 1.0, 0.0))
             put(ftab, 2 * base + 1, jnp.where(add(col == s, 1, 0) > 0, 1.0, 0.0))
 
 
 def kernel(n, side, ndp, cap, kk, tbd, sbd, chunk, nk, c0,
            dest_ref, mask_ref, t_hbm, s_hbm, w_hbm, loss_ref, mean_ref,
-           itab, ftab, ivec, fvec, tbuf, stbuf, wbuf, prob, sbuf, rb00, rb01, rb10, rb11, pscan, pown, dsnd, drcv,
-           st_send, st_recv, tr, scl, smx, tot, inv, ftr, fsend, frecv, dsend, drecv,
+           stab, itab, ftab, svec, ivec, fvec, tbuf, stbuf, wbuf, prob, sbuf, rb00, rb01, rb10, rb11, pscan, pown, dsnd, drcv,
+           st_send, st_recv, tr, scl, smx, inv, ftr, fsend, frecv, dsend, drecv,
            in_sem, w_sem, rs_sem, rr_sem, ds_sem, dr_sem, sts_sem, str_sem,
            fs_sem, fr_sem, es_sem, er_sem, credit, dcredit):
     half = chunk // 2
@@ -183,6 +198,11 @@
             send_sem=sts_sem.at[0, 0], recv_sem=str_sem.at[k, src],
             device_id={"vocab": src}).wait_recv()
 
+    def fin_copy(r, d, src):
+        return pltpu.make_async_remote_copy(
+            src_ref=fsend.at[r], dst_ref=frecv.at[src, r], send_sem=fs_sem.at[r, d],
+            recv_sem=fr_sem.at[r, src], device_id={"vocab": d})
+
     def cols(b):
         return pl.ds(pl.multiple_of(b * BLOCK, BLOCK), BLOCK)
 
@@ -206,9 +226,9 @@
     def bcast(column, to=shape):
         return jnp.broadcast_to(column, to)
 
-    load_t(0).start()
     for q in range(wp):
         load_w(q).start()
+    load_t(0).start()
 
     barrier = pltpu.get_barrier_semaphore()
     for d in peers:
@@ -217,12 +237,25 @@
         pl.semaphore_signal(barrier, inc=1, device_id={"dp": e})
     tr[...] = jnp.zeros_like(tr)
     ftr[...] = jnp.zeros_like(ftr)
+    svec[...] = jnp.zeros_like(svec)
     ivec[...] = jnp.zeros_like(ivec)
     fvec[...] = jnp.zeros_like(fvec)
-    build_tables(n, side, cap, kk, tbd, sbd, y, x, c, me, dest_ref, ivec, fvec)
-    to_smem = [pltpu.make_async_copy(ivec, itab, in_sem.at[2]), pltpu.make_async_copy(fvec, ftab, in_sem.at[3])]
-    for copy in to_smem:
-        copy.start()
+    send_table(n, cap, kk, tbd, sbd, me, dest_ref, svec)
+    send_copy = pltpu.make_async_copy(svec, stab, in_sem.at[2])
+    send_copy.start()
+    receive_copies = [pltpu.make_async_copy(ivec, itab, in_sem.at[3]), pltpu.make_async_copy(fvec, ftab, in_sem.at[4])]
+
+    def weight_sums(p, carry):
+        for j in range(batch):
+            b = p * batch + j
+            whole = sum(wbuf[b * kk + i].astype(F32) for i in range(kk))
+            inv[pl.ds(b, 1), :] = 1.0 / jnp.sum(whole.T, axis=0, keepdims=True)
+        return carry
+
+    for q in range(wp):
+        load_w(q).wait()
+        lax.fori_loop(edges[q], edges[q + 1], weight_sums, 0)
+    send_copy.wait()
     pl.semaphore_wait(barrier, n + ndp - 2)
 
     def produce(k, par):
@@ -238,44 +271,15 @@
             prob[b] = (e * inv[pl.ds(b, 1), :]).astype(BF16)
             return total + e
 
-        @pl.when(k == 0)
-        def _():
-            ones = jnp.ones((kk * BLOCK, BLOCK), BF16)
-            square = (BLOCK, BLOCK)
-            diag = lax.broadcasted_iota(jnp.int32, square, 0) == lax.broadcasted_iota(jnp.int32, square, 1)
-
-            def both(p, total):
-                blocks = [p * batch + j for j in range(batch)]
-                wide = jnp.concatenate([
-                    jnp.concatenate([wbuf[b * kk + j] for j in range(kk)], axis=1) for b in blocks], axis=0)
-                sums = jnp.dot(wide, ones, preferred_element_type=F32)
-                for j, b in enumerate(blocks):
-                    own = jnp.where(diag, sums[j * BLOCK:(j + 1) * BLOCK], 0.0)
-                    inv[pl.ds(b, 1), :] = 1.0 / jnp.sum(own, axis=0, keepdims=True)
-                for b in blocks:
-                    total = expo(b, total)
-                return total
-
-            total = zeros
-            for q in range(wp):
-                load_w(q).wait()
-                total = lax.fori_loop(edges[q], edges[q + 1], both, total)
-            tot[...] = total
-            load_s(0).start()
-            for copy in to_smem:
-                copy.wait()
-
-        @pl.when(k > 0)
-        def _():
-            tot[...] = lax.fori_loop(0, tbd, expo, zeros, unroll=4)
+        total = lax.fori_loop(0, tbd, expo, zeros, unroll=4)
 
         @pl.when(k + 1 < nk)
         def _():
             load_t(k + 1).start()
 
-        tsum = bcast(jnp.sum(tot[...], axis=1, keepdims=True))
+        tsum = bcast(jnp.sum(total, axis=1, keepdims=True))
         stat = jnp.where(lane == 0, tmax, jnp.where(lane == 1, tsum, 0.0))
-        stat = jnp.concatenate([stat, jnp.zeros((BLOCK - chunk, BLOCK), F32)], axis=0).T[:8]
+        stat = jnp.concatenate([stat, jnp.zeros((BLOCK - chunk, BLOCK), F32)], axis=0).T[:2]
         st_send[k] = stat
         st_recv[k, me] = stat
 
@@ -303,8 +307,8 @@
                     dst.append(rbuf[par][h].at[place(h, mine[h], parts(h, o)[1])])
 
             def one(r):
-                i = itab[0, d * cap + r]
-                b = itab[1, d * cap + r]
+                i = stab[0, d * cap + r]
+                b = stab[1, d * cap + r]
                 res = jnp.dot(prob[b], wbuf[i], preferred_element_type=F32).astype(BF16)
                 dst[0][r] = res[:half]
                 dst[1][r] = res[half:]
@@ -328,7 +332,7 @@
         columns = []
         for g in range(groups):
             for j in range(min(per, n - g * per)):
-                tr[j * 8:j * 8 + 8, :] = st_recv[k, g * per + j]
+                tr[j * 8:j * 8 + 2, :] = st_recv[k, g * per + j]
             block = tr[...].T
             for j in range(min(per, n - g * per)):
                 columns.append((block[:chunk, 8 * j:8 * j + 1], block[:chunk, 8 * j + 1:8 * j + 2]))
@@ -338,7 +342,7 @@
             scl[j] = bcast(jnp.exp(m - gmax) / gsum)
 
         def scan(h, rel, dst):
-            base = 2 + 3 * (h * side + rel)
+            base = 3 * (h * side + rel)
             fbase = 2 * (h * side + rel)
 
             def step(i, acc):
@@ -361,7 +365,7 @@
                 base = h * side + r
 
                 def pick(s, carry):
-                    dsnd[par, h, r - 1, s] = (pscan[itab[4 + 3 * base, s]] * ftab[2 * base + 1, s]).astype(BF16)
+                    dsnd[par, h, r - 1, s] = (pscan[itab[2 + 3 * base, s]] * ftab[2 * base + 1, s]).astype(BF16)
                     return carry
                 for q in range(npc):
                     lax.fori_loop(q * piece, (q + 1) * piece, pick, 0, unroll=4)
@@ -394,7 +398,7 @@
 
                 def step(s, carry):
                     tot, kla = carry
-                    acc = pown[par, h, itab[4 + 3 * base, s]] * ftab[2 * base + 1, s]
+                    acc = pown[par, h, itab[2 + 3 * base, s]] * ftab[2 * base + 1, s]
                     for r in range(1, side):
                         acc = acc + drcv[par, h, r - 1, s].astype(F32)
                     tgt = (1.0 - SMOOTH) * acc + c0
@@ -421,7 +425,13 @@
                     pl.semaphore_signal(dcredit.at[h, r - 1], inc=1, device_id={"vocab": along(h, side - r)})
         per = BLOCK // chunk
         ftr[pl.ds(pl.multiple_of(lax.rem(k, per) * chunk, chunk), chunk), :] = jnp.concatenate(pieces, axis=0)
-        fsend[k // per] = ftr[...].T[:8]
+
+        @pl.when(lax.rem(k, per) == per - 1)
+        def _():
+            r = k // per
+            fsend[r] = ftr[...].T[:4]
+            for j in range(n - 1):
+                fin_copy(r, peers[j], me).start()
 
     def pair(j, carry):
         for par in range(2):
@@ -430,6 +440,16 @@
             @pl.when(it < nk)
             def _():
                 produce(it, par)
+
+            if par == 0:
+                @pl.when(it == 0)
+                def _():
+                    load_s(0).start()
+                    receive_tables(n, side, cap, kk, tbd, sbd, y, x, c, dest_ref, ivec, fvec)
+                    for copy in receive_copies:
+                        copy.start()
+                    for copy in receive_copies:
+                        copy.wait()
 
             @pl.when((it >= 3) & (it <= nk + 2))
             def _():
@@ -442,23 +462,16 @@
 
     lax.fori_loop(0, (nk + 4) // 2, pair, 0)
 
-    def fin_copy(d, src):
-        return pltpu.make_async_remote_copy(
-            src_ref=fsend, dst_ref=frecv.at[src], send_sem=fs_sem.at[d],
-            recv_sem=fr_sem.at[src], device_id={"vocab": d})
-
     def dp_copy(e, src):
         return pltpu.make_async_remote_copy(
             src_ref=dsend, dst_ref=drecv.at[src], send_sem=es_sem.at[e],
             recv_sem=er_sem.at[src], device_id={"dp": e})
 
-    for d in peers:
-        fin_copy(d, me).start()
     frecv[me] = fsend[...]
-    for d in peers:
-        fin_copy(d, d).wait_recv()
     dsend[...] = jnp.zeros_like(dsend)
     for r in range(nk * chunk // BLOCK):
+        for d in peers:
+            fin_copy(r, d, d).wait_recv()
         parts_ = [frecv[v, r] for v in range(n)]
         gmax = functools.reduce(jnp.maximum, [p[2:3] for p in parts_])
         lse = gmax + jnp.log(sum(p[3:4] * jnp.exp(p[2:3] - gmax) for p in parts_))
@@ -477,8 +490,9 @@
     mean_ref[...] = jnp.broadcast_to(
         jnp.sum(sums[0:1], axis=1, keepdims=True) / jnp.sum(sums[1:2], axis=1, keepdims=True),
         (8, BLOCK))
-    for d in peers:
-        fin_copy(d, d).wait_send()
+    for r in range(nk * chunk // BLOCK):
+        for d in peers:
+            fin_copy(r, d, d).wait_send()
     for e in dp_peers:
         dp_copy(e, e).wait_send()
     for k in range(max(nk - 2, 0), nk):
@@ -508,8 +522,8 @@
     nk = rows // chunk
     c0 = SMOOTH / (sbd * BLOCK * n)
     width = -(-max(n * cap, sbd) // BLOCK) * BLOCK
-    itab, ftab = (2 + 6 * side, width), (4 * side, width)
-    dest = tile_dest.T.reshape(kk, n, tbd)
+    stab, itab, ftab = (2, width), (6 * side, width), (4 * side, width)
+    dest = tile_dest.T
     weights = tile_weight.reshape(tbd * kk, BLOCK, BLOCK)
     anyspec = pl.BlockSpec(memory_space=pl.ANY)
     vmem = pl.BlockSpec(memory_space=pltpu.VMEM)
@@ -523,8 +537,8 @@
         in_specs=[vmem] * 2 + [anyspec] * 3,
         out_specs=[vmem] * 2,
         scratch_shapes=[
-            pltpu.SMEM(itab, jnp.int32), pltpu.SMEM(ftab, F32),
-            pltpu.VMEM(itab, jnp.int32), pltpu.VMEM(ftab, F32),
+            pltpu.SMEM(stab, jnp.int32), pltpu.SMEM(itab, jnp.int32), pltpu.SMEM(ftab, F32),
+            pltpu.VMEM(stab, jnp.int32), pltpu.VMEM(itab, jnp.int32), pltpu.VMEM(ftab, F32),
             pltpu.VMEM((chunk, tbd * BLOCK), BF16),
             pltpu.VMEM((chunk, sbd * BLOCK), BF16),
             pltpu.VMEM((tbd * kk, BLOCK, BLOCK), BF16),
@@ -535,23 +549,22 @@
             pltpu.VMEM((2, 2, group * cap, half, BLOCK), F32),
             pltpu.VMEM((2, 2, side - 1, sbd, half, BLOCK), BF16),
             pltpu.VMEM((2, 2, side - 1, sbd, half, BLOCK), BF16),
-            pltpu.VMEM((nk, 8, BLOCK), F32),
-            pltpu.VMEM((nk, n, 8, BLOCK), F32),
+            pltpu.VMEM((nk, 2, BLOCK), F32),
+            pltpu.VMEM((nk, n, 2, BLOCK), F32),
             pltpu.VMEM((BLOCK, BLOCK), F32),
             pltpu.VMEM((n, chunk, BLOCK), F32),
             pltpu.VMEM((chunk, BLOCK), F32),
-            pltpu.VMEM((chunk, BLOCK), F32),
             pltpu.VMEM((tbd, BLOCK), F32),
             pltpu.VMEM((BLOCK, BLOCK), F32),
-            pltpu.VMEM((rows // BLOCK, 8, BLOCK), F32),
-            pltpu.VMEM((n, rows // BLOCK, 8, BLOCK), F32),
+            pltpu.VMEM((rows // BLOCK, 4, BLOCK), F32),
+            pltpu.VMEM((n, rows // BLOCK, 4, BLOCK), F32),
             pltpu.VMEM((8, BLOCK), F32),
             pltpu.VMEM((ndp, 8, BLOCK), F32),
-            dma((4,)), dma((4,)),
+            dma((5,)), dma((4,)),
             dma((2, 2, n - side)), dma((2, 2, group * side)),
             dma((2, 2, side - 1, 4)), dma((2, 2, side - 1, 4)),
             dma((2, n - 1)), dma((nk, n)),
-            dma((n,)), dma((n,)), dma((ndp,)), dma((ndp,)),
+            dma((rows // BLOCK, n)), dma((rows // BLOCK, n)), dma((ndp,)), dma((ndp,)),
             reg((2, group)), reg((2, side - 1)),
         ],
         compiler_params=pltpu.CompilerParams(

time: 325 us -> 318 us (0.978)
  Pallas kernels: 320 us -> 315 us
    pallas_call x1, Pallas kernels: 320 us -> 315 us  [local(): pl.pallas_call(functools.partial(kernel, n, side, ndp, cap, kk, tbd, sbd,...]
where the time goes in v3:
time: 318 us
  Pallas kernels  315 us (99%)
    pallas_call x1, Pallas kernels, local(): pl.pallas_call(functools.partial(kernel, n, side, ndp, cap, kk, tbd, sbd,...  315 us

profile of v3, /device:TPU:0, one launch (start us, length us, event | category | flops | bytes accessed | tf_op | source)
XLA Modules:
  0.0 317.6 jit_solution(7622774594345056849)
XLA Ops:
  0.6 314.5 %shard_map.68 = (f32[3,128]{1,0:T(4,128)}, f32[8,128]{1,0:T(8,128)}) custom-call(s32[2,1184]{1,0:T(2,128)} %bitcast.6, s32[3,128]{1,0:T(4,128)} %bitcast.8, bf16[384,18944]{1,0:T(8,128)(2,1)} %t_hbm.1, bf16[384,15872]{1,0:T(8,128)(2,1)} %s_hbm.1, bf16[296,128,128]{2,1,0:T(8,128)(2,1)} %bitcast.5), custom_call_target="tpu_custom_call" | custom-call | tf_op jit(solution)/shard_map/pallas_call | solution.py:534
  315.2 1.2 slice.3
  316.4 1.2 copy.8
